TPU v7x, 512 devices: a whole 4x4x16 slice. The times are simulated.
512 devices in a mesh: freq: 4 (over x), row: 16 (over y, z_hi, core), col: 8 (over z_lo).
Axes of the slice: x: 4, y: 4, z: 16 (z_hi: 2, z_lo: 8; z = z_hi * 8 + z_lo), core: 2. Of those that a mesh axis runs over, the one named last changes fastest.
Arguments:
- pair_block: bfloat16 [768, 8192], P('freq', 'row'), may hold values from -6 to 6
- screened: bfloat16 [16, 8192, 8192], P('freq', 'row', 'col'), may hold values from -0.0625 to 0.0625
- pair_gaps: float32 [768], replicated, may hold values from 0.5 to 4
- omega_values: float32 [16], replicated, may hold values from 0.25 to 8
- quad_weight: float32 [16], replicated, may hold values from 0.2 to 1
- freq_slot: int32 [16], replicated, may hold values from 0 to 15, each once
- block_list: int32 [64], replicated, may hold values from 0 to 63, each once
Outputs:
- gamma: float32 [768, 8192], P(('freq', 'row'), 'col')
Inputs may be any that keep to these rules, and one draw needn't show every extreme that they name: `freq_slot`: a permutation of the frequencies. `block_list`: a permutation of the blocks.
All inputs are finite; a program needn't handle non-finite values.
Results may differ from a plain program's by a relative error of at most 0.0003.
Values may be sent and summed in bfloat16 or wider, within the bound.
A program may use at most 64 MiB of HBM per device.

v0:
```python
import jax
import jax.numpy as jnp
from jax import lax
from jax.sharding import PartitionSpec as P


def laid_out(parts, dim):
    shape = list(parts.shape[1:])
    shape[dim] *= parts.shape[0]
    return jnp.moveaxis(parts, 0, dim).reshape(shape)


def copy_for_each(array, axis):
    copies = jnp.broadcast_to(array, (lax.axis_size(axis), *array.shape))
    return lax.all_to_all(copies, axis, split_axis=0, concat_axis=0, tiled=True)


def gather_directly(array, axis, dim):
    return laid_out(copy_for_each(array, axis), dim)


def split_up(array, dim, peers):
    shape = array.shape
    parts = array.reshape(*shape[:dim], peers, shape[dim] // peers, *shape[dim + 1 :])
    return jnp.moveaxis(parts, dim, 0)


def summed_on_arrival(array, axis, dim):
    parts = split_up(array, dim, lax.axis_size(axis))
    arrived = lax.all_to_all(parts, axis, split_axis=0, concat_axis=0, tiled=True)
    return arrived.sum(axis=0)


def local(pair_block, screened, pair_gaps, omega_values, quad_weight, freq_slot, block_list):
    blocks_all = block_list.shape[0]
    rows_each = pair_gaps.shape[0] // blocks_all
    matches = block_list[:, None] == jnp.arange(blocks_all, dtype=jnp.int32)[None, :]
    gap_table = pair_gaps.reshape(blocks_all, rows_each)
    gap_rows = jnp.sum(jnp.where(matches[:, :, None], gap_table[None, :, :], 0.0), axis=1).reshape(
        -1
    )
    slots_all = freq_slot.shape[0]
    slot_match = freq_slot[:, None] == jnp.arange(slots_all, dtype=jnp.int32)[None, :]
    omega_slot = jnp.sum(jnp.where(slot_match, omega_values[None, :], 0.0), axis=1)
    weight_slot = jnp.sum(jnp.where(slot_match, quad_weight[None, :], 0.0), axis=1)
    freq_dev = screened.shape[0]
    first_slot = lax.axis_index("freq") * freq_dev
    omega_mine = lax.dynamic_slice_in_dim(omega_slot, first_slot, freq_dev)
    weight_mine = lax.dynamic_slice_in_dim(weight_slot, first_slot, freq_dev)
    factor = (
        weight_mine[:, None]
        * 2.0
        * gap_rows[None, :]
        / (gap_rows[None, :] ** 2 + omega_mine[:, None] ** 2)
    )
    gathered = gather_directly(pair_block, "freq", 0)
    row_groups = lax.axis_size("row")
    columns_here = screened.shape[2]
    running = jnp.zeros((rows_each * row_groups * lax.axis_size("freq"), columns_here), jnp.float32)
    for member in range(freq_dev):
        product = jnp.dot(gathered, screened[member], preferred_element_type=jnp.float32)
        running = running + factor[member][:, None] * product
    halfway = summed_on_arrival(running, "freq", 0)
    result = summed_on_arrival(halfway, "row", 0)
    return result


def solution(mesh):
    placed = (P("freq", "row"), P("freq", "row", "col"), P(), P(), P(), P(), P())
    return jax.shard_map(
        local, mesh=mesh, in_specs=placed, out_specs=P(("freq", "row"), "col"), check_vma=False
    )
```

profile of v0, /device:TPU:32, one launch (start us, length us, event | category | flops | bytes accessed | tf_op | source)
XLA Modules:
  0.0 142.1 jit_solution(5748609683067424174)
XLA Ops:
  0.0 1.9 %broadcast_in_dim.59 = bf16[4,192,512]{2,1,0:T(8,128)(2,1)} broadcast(bf16[192,512]{1,0:T(8,128)(2,1)} %param.7), dimensions={1,2} | broadcast | bytes 983040 | tf_op jit(solution)/shard_map/broadcast_in_dim | solution.py:14
  1.9 4.3 %all-to-all-start = ((bf16[4,192,512]{2,1,0:T(8,128)(2,1)}), bf16[4,192,512]{2,1,0:T(8,128)(2,1)S(1)}, u32[]{:S(2)}, u32[]{:S(2)}) async-start(bf16[4,192,512]{2,1,0:T(8,128)(2,1)} %broadcast_in_dim.59), calls=%async_computation | async-start | bytes 1572864 | tf_op jit(solution)/shard_map/all_to_all | solution.py:15
  6.2 0.7 iota_compare_fusion
  6.9 0.8 broadcast_in_dim.55
  7.7 0.1 copy.8
  7.8 0.2 select_reduce_fusion
  7.9 0.1 copy.9
  8.0 0.1 mul.65
  8.2 0.9 select_reduce_fusion.2
  9.0 0.1 dynamic-slice_multiply_fusion
  9.1 0.1 add_divide_fusion
  9.2 9.2 %all-to-all-done = bf16[4,192,512]{2,1,0:T(8,128)(2,1)S(1)} async-done(((bf16[4,192,512]{2,1,0:T(8,128)(2,1)}), bf16[4,192,512]{2,1,0:T(8,128)(2,1)S(1)}, u32[]{:S(2)}, u32[]{:S(2)}) %all-to-all-start) | async-done | bytes 786464 | tf_op jit(solution)/shard_map/all_to_all | solution.py:15
  18.4 0.0 copy-start
  18.4 2.4 %fusion.1 = f32[768,1024]{1,0:T(8,128)S(1)} fusion(bf16[768,512]{1,0:T(8,128)(2,1)S(1)} %bitcast.18, bf16[4,512,1024]{2,1,0:T(8,128)(2,1)} %param.8), kind=kOutput, calls=%fused_computation.2 | convolution fusion | flops 805306368 | bytes 4980736 | tf_op jit(solution)/shard_map/dot_general | solution.py:61
  20.8 0.1 copy-done
  20.9 1.0 fusion.3
  21.9 1.0 fusion.5
  22.9 1.2 multiply_add_fusion
  24.1 39.2 %all_to_all.15 = f32[4,192,1024]{2,1,0:T(8,128)S(1)} all-to-all(f32[4,192,1024]{2,1,0:T(8,128)S(1)} %bitcast.22), channel_id=1, replica_groups=mesh['freq'=4,'row'=16,'col'=8] {'freq'}, dimensions={0} | all-to-all | bytes 6291456 | tf_op jit(solution)/shard_map/all_to_all | solution.py:30
  63.3 1.2 reduce_sum.48
  64.5 1.2 reshape.52
  65.7 75.6 %all_to_all.16 = f32[16,12,1024]{2,1,0:T(8,128)S(1)} all-to-all(f32[16,12,1024]{2,1,0:T(8,128)S(1)} %reshape.52), channel_id=1, replica_groups=mesh['freq'=4,'row'=16,'col'=8] {'row'}, dimensions={0} | all-to-all | bytes 1572864 | tf_op jit(solution)/shard_map/all_to_all | solution.py:30
  141.4 0.7 reduce_sum.49
  (2 shorter events, 0.0 us)
Async XLA Ops:
  1.9 16.6 %all-to-all-start = ((bf16[4,192,512]{2,1,0:T(8,128)(2,1)}), bf16[4,192,512]{2,1,0:T(8,128)(2,1)S(1)}, u32[]{:S(2)}, u32[]{:S(2)}) async-start(bf16[4,192,512]{2,1,0:T(8,128)(2,1)} %broadcast_in_dim.59), calls=%async_computation | async-start | bytes 1572864 | tf_op jit(solution)/shard_map/all_to_all | solution.py:15
  18.4 2.5 %copy-start = (bf16[4,512,1024]{2,1,0:T(8,128)(2,1)S(1)}, bf16[4,512,1024]{2,1,0:T(8,128)(2,1)}, u32[]{:S(2)}) copy-start(bf16[4,512,1024]{2,1,0:T(8,128)(2,1)} %param.8) | copy-start | bytes 12582916
where the time goes:
time: 142 us
  blocking collectives  115 us (81%)
  waiting for transfers between devices  9.2 us (6%)
  matrix products  5.48 us (4%)
  local copies, waits for them, and re-layouts  4.32 us (3%)
  starting transfers between devices  4.29 us (3%)
  other arithmetic  3.84 us (3%)
    all_to_all x2, blocking collectives, summed_on_arrival(): lax.all_to_all(parts, axis, split_axis=0, concat_axis=0, tiled=True)  115 us
    all_to_all x1, waiting for transfers between devices, copy_for_each(): return lax.all_to_all(copies, axis, split_axis=0, concat_axis=0, tiled=True)  9.2 us
    dot_general x4, matrix products, local(): jnp.dot(gathered, screened[member], preferred_element_type=jnp.float32)  5.48 us
    all_to_all x1, starting transfers between devices, copy_for_each(): return lax.all_to_all(copies, axis, split_axis=0, concat_axis=0, tiled=True)  4.29 us
  transfers between devices with their start and end apart: 1, of which 1 were waited for; matrix products, arithmetic and copies ran while one was open for 2% of the time, Pallas kernels for 0%

commit v1 on v0

v1 whole, which is shorter than its diff:
```python
import jax
import jax.numpy as jnp
from jax import lax
from jax.experimental import pallas as pl
from jax.experimental.pallas import tpu as pltpu
from jax.sharding import PartitionSpec as P

MESH = pl.DeviceIdType.MESH
F32 = jnp.float32


def kernel(
    b_hbm, w_hbm, gaps_hbm, omega_hbm, weight_hbm, slot_hbm, list_hbm, out_ref,
    b_own, w_ref, gaps, omega, weight, slot, blist, in_sem,
    rows_ref, fac_ref, bg, part, part_in, ys, yr, xs, xr, zs, zr,
    g_send, g_recv, d_send, d_recv, y_send, y_recv, x_send, x_recv, z_send, z_recv,
):
    f, r, c = lax.axis_index("freq"), lax.axis_index("row"), lax.axis_index("col")
    y, zh, core = r // 4, (r // 2) % 2, r % 2
    slots = w_ref.shape[0]

    def at_x(k):
        return ((f + k) % 4, r, c)

    def at_y(k):
        return (f, (r + 4 * k) % 16, c)

    partner = (f, r + 1 - 2 * core, c)
    across = (f, r + 2 - 4 * zh, c)

    barrier = pltpu.get_barrier_semaphore()
    peers = [at_x(1), at_x(3), at_x(2), at_y(1), at_y(3), at_y(2), partner, across]
    for peer in peers:
        pl.semaphore_signal(barrier, inc=1, device_id=peer, device_id_type=MESH)

    small = [
        pltpu.make_async_copy(src, dst, in_sem.at[i])
        for i, (src, dst) in enumerate(
            ((list_hbm, blist), (gaps_hbm, gaps), (slot_hbm, slot), (omega_hbm, omega), (weight_hbm, weight))
        )
    ]
    own = pltpu.make_async_copy(b_hbm, b_own, in_sem.at[5])
    heavy = [pltpu.make_async_copy(w_hbm.at[s], w_ref.at[s], in_sem.at[6 + s]) for s in range(slots)]
    own.start()
    for copy in small + heavy:
        copy.start()

    to = lax.broadcasted_iota(jnp.int32, (192, 192), 0)
    source = lax.broadcasted_iota(jnp.int32, (192, 192), 1)
    half_of = (to >= 96).astype(jnp.int32)
    in_half = to - 96 * half_of
    core_of = (in_half >= 48).astype(jnp.int32)
    in_core = in_half - 48 * core_of
    tail = in_core - 32
    wide_y, wide_i = lax.shift_right_logical(in_core, 3), lax.bitwise_and(in_core, 7)
    tail_y, tail_i = lax.shift_right_logical(jnp.maximum(tail, 0), 2), 8 + lax.bitwise_and(jnp.maximum(tail, 0), 3)
    y_of = jnp.where(tail >= 0, tail_y, wide_y)
    i_of = jnp.where(tail >= 0, tail_i, wide_i)
    z_of = jnp.where(half_of == 0, 1 - zh, zh)
    wanted = y_of * 48 + z_of * 24 + core_of * 12 + i_of
    permute = jnp.where(source == wanted, 1.0, 0.0).astype(jnp.bfloat16)
    own.wait()
    bg[0] = jnp.dot(permute, b_own[...], preferred_element_type=F32).astype(jnp.bfloat16)

    pl.semaphore_wait(barrier, len(peers))

    def gather(k, half):
        rows = pl.ds(96 * half, 96)
        return pltpu.make_async_remote_copy(
            src_ref=bg.at[0, rows], dst_ref=bg.at[k, rows], send_sem=g_send.at[2 * k + half],
            recv_sem=g_recv.at[2 * k + half], device_id=at_x(k), device_id_type=MESH,
        )

    gathers = {(k, half): gather(k, half) for half in range(2) for k in (1, 3, 2)}
    for k in (1, 3, 2):
        gathers[k, 0].start()

    for copy in small:
        copy.wait()

    def fill(n, carry):
        k, half, of_core, of_y = n // 16, (n // 8) % 2, (n // 4) % 2, n % 4
        z = jnp.where(half == 0, 1 - zh, zh)
        block = blist[((f + 4 - k) % 4) * 16 + of_y * 4 + z * 2 + of_core]
        for i in range(12):
            row = of_core * 48 + (of_y * 8 + i if i < 8 else 32 + of_y * 4 + i - 8)
            rows_ref[2 * k + half, pl.ds(row, 1), :] = jnp.full((1, 128), gaps[block * 12 + i], F32)
        return carry

    lax.fori_loop(0, 64, fill, 0)

    def weigh(n, carry):
        gap = rows_ref[n]
        for s in range(slots):
            held = slot[f * slots + s]
            fac_ref[s, n] = weight[held] * 2.0 * gap / (gap * gap + omega[held] * omega[held])
        return carry

    lax.fori_loop(0, 8, weigh, 0)
    for copy in heavy:
        copy.wait()

    def compute(k, half):
        left = bg[k, pl.ds(96 * half, 96), :]

        def tile(n, carry):
            columns = pl.ds(pl.multiple_of(n * 256, 256), 256)
            total = None
            for s in range(slots):
                product = jnp.dot(left, w_ref[s, :, columns], preferred_element_type=F32)
                factor = fac_ref[s, 2 * k + half]
                term = product * jnp.concatenate([factor, factor], axis=1)
                total = term if total is None else total + term
            part[2 * k + half, :, columns] = total
            return carry

        lax.fori_loop(0, w_ref.shape[2] // 256, tile, 0)

    def swap(k, half):
        n = 2 * k + half
        return pltpu.make_async_remote_copy(
            src_ref=part.at[n, pl.ds(pl.multiple_of(48 - 48 * core, 8), 48)], dst_ref=part_in.at[n],
            send_sem=d_send.at[n], recv_sem=d_recv.at[n], device_id=partner, device_id_type=MESH,
        )

    def along_y(k, half, j):
        n = 2 * k + half
        return pltpu.make_async_remote_copy(
            src_ref=ys.at[n, (y + j) % 4], dst_ref=yr.at[n, j - 1], send_sem=y_send.at[n, j - 1],
            recv_sem=y_recv.at[n, j - 1], device_id=at_y(j), device_id_type=MESH,
        )

    def along_x(k, half):
        n = 2 * k + half
        return pltpu.make_async_remote_copy(
            src_ref=xs.at[n], dst_ref=xr.at[n], send_sem=x_send.at[n],
            recv_sem=x_recv.at[n], device_id=at_x(4 - k), device_id_type=MESH,
        )

    low = lax.broadcasted_iota(jnp.int32, (8, 512), 0) < 4

    def to_y(k, half):
        n = 2 * k + half
        swap(k, half).wait_recv()
        both = part[n, pl.ds(pl.multiple_of(48 * core, 8), 48), :] + part_in[n]
        for d in range(4):
            ys[n, d, 0:8] = both[8 * d : 8 * d + 8, :512]
            ys[n, d, 8:16] = both[8 * d : 8 * d + 8, 512:]
            mixed = both[32 + 8 * (d // 2) : 40 + 8 * (d // 2)]
            if d % 2 == 0:
                ys[n, d, 16:24] = jnp.where(low, mixed[:, :512], pltpu.roll(mixed[:, 512:], 4, 0))
            else:
                ys[n, d, 16:24] = jnp.where(low, pltpu.roll(mixed[:, :512], 4, 0), mixed[:, 512:])
        for j in (1, 3, 2):
            along_y(k, half, j).start()

    def to_x(k, half):
        n = 2 * k + half
        for j in (1, 3, 2):
            along_y(k, half, j).wait_recv()
        xs[n] = (ys[n, y] + yr[n, 0]) + (yr[n, 1] + yr[n, 2])
        if k:
            along_x(k, half).start()

    def arrived(half):
        for k in (1, 3, 2):
            along_x(k, half).wait_recv()
        return (xs[half] + xr[2 + half]) + (xr[4 + half] + xr[6 + half])

    def begin(k, half):
        if k:
            gathers[k, half].wait_recv()
        compute(k, half)
        swap(k, half).start()

    begin(0, 0)
    begin(1, 0)
    to_y(0, 0)
    begin(3, 0)
    to_y(1, 0)
    begin(2, 0)
    to_y(3, 0)
    for k in (1, 3, 2):
        gathers[k, 1].start()
    to_y(2, 0)
    to_x(0, 0)
    to_x(1, 0)
    begin(0, 1)
    to_x(3, 0)
    to_x(2, 0)
    zs[...] = arrived(0)
    over = pltpu.make_async_remote_copy(
        src_ref=zs, dst_ref=zr, send_sem=z_send, recv_sem=z_recv, device_id=across, device_id_type=MESH
    )
    over.start()
    to_y(0, 1)
    begin(1, 1)
    begin(3, 1)
    to_y(1, 1)
    begin(2, 1)
    to_y(3, 1)
    to_y(2, 1)
    for k in (0, 1, 3, 2):
        to_x(k, 1)
    kept = arrived(1)
    over.wait_recv()
    total = kept + zr[...]
    out_ref[0:8, :512] = total[0:8]
    out_ref[0:8, 512:] = total[8:16]
    out_ref[8:12, :512] = total[16:20]
    out_ref[8:12, 512:] = pltpu.roll(total[16:24], 4, 0)[0:4]

    for half in range(2):
        for k in range(4):
            swap(k, half).wait_send()
            for j in (1, 2, 3):
                along_y(k, half, j).wait_send()
            if k:
                gathers[k, half].wait_send()
                along_x(k, half).wait_send()
    over.wait_send()


def local(*args):
    dma = pltpu.SemaphoreType.DMA
    hbm = pl.BlockSpec(memory_space=pl.ANY)
    pair_block, screened, pair_gaps, omega_values, quad_weight, freq_slot, block_list = args
    scratch = [
        pltpu.VMEM(pair_block.shape, jnp.bfloat16),
        pltpu.VMEM(screened.shape, jnp.bfloat16),
        pltpu.SMEM(pair_gaps.shape, F32),
        pltpu.SMEM(omega_values.shape, F32),
        pltpu.SMEM(quad_weight.shape, F32),
        pltpu.SMEM(freq_slot.shape, jnp.int32),
        pltpu.SMEM(block_list.shape, jnp.int32),
        dma((10,)),
        pltpu.VMEM((8, 96, 128), F32),
        pltpu.VMEM((4, 8, 96, 128), F32),
        pltpu.VMEM((4, 192, 512), jnp.bfloat16),
        pltpu.VMEM((8, 96, 1024), F32),
        pltpu.VMEM((8, 48, 1024), F32),
        pltpu.VMEM((8, 4, 24, 512), F32),
        pltpu.VMEM((8, 3, 24, 512), F32),
        pltpu.VMEM((8, 24, 512), F32),
        pltpu.VMEM((8, 24, 512), F32),
        pltpu.VMEM((24, 512), F32),
        pltpu.VMEM((24, 512), F32),
        dma((8,)), dma((8,)), dma((8,)), dma((8,)), dma((8, 3)), dma((8, 3)), dma((8,)), dma((8,)),
        dma, dma,
    ]
    return pl.pallas_call(
        kernel,
        out_shape=jax.ShapeDtypeStruct((12, 1024), F32),
        in_specs=[hbm] * 7,
        out_specs=pl.BlockSpec(memory_space=pltpu.VMEM),
        scratch_shapes=scratch,
        compiler_params=pltpu.CompilerParams(collective_id=0, has_side_effects=True),
        name="rpa_exchange",
    )(*args)


def solution(mesh):
    placed = (P("freq", "row"), P("freq", "row", "col"), P(), P(), P(), P(), P())
    return jax.shard_map(
        local, mesh=mesh, in_specs=placed, out_specs=P(("freq", "row"), "col"), check_vma=False
    )
```

time: 142 us -> 56.2 us (0.40)
  the two profiles are of different devices: /device:TPU:32 before, /device:TPU:1 now
where the time goes in v1:
time: 56.2 us; the launch traced here: 56.1 us
  Pallas kernels  54.6 us (97%)
  local copies, waits for them, and re-layouts  1.47 us (3%)
    pallas_call x1, Pallas kernels, local(): pl.pallas_call(kernel, out_shape=jax.ShapeDtypeStruct((12, 1024), F32), i...  54.6 us
    unnamed x1, local copies, waits for them, and re-layouts  1.47 us

profile of v1, /device:TPU:1, one launch (start us, length us, event | category | flops | bytes accessed | tf_op | source)
XLA Modules:
  0.0 56.1 jit_solution(15364847454503941501)
XLA Ops:
  0.0 54.6 %rpa_exchange.1 = f32[12,1024]{1,0:T(8,128)} custom-call(bf16[192,512]{1,0:T(8,128)(2,1)} %b_hbm.1, bf16[4,512,1024]{2,1,0:T(8,128)(2,1)} %w_hbm.1, f32[768]{0:T(1024)} %gaps_hbm.1, f32[16]{0:T(128)} %omega_hbm.1, f32[16]{0:T(128)} %weight_hbm.1, s32[16]{0:T(128)} %slot_hbm.1, s32[64]{0:T(128)} %list_hbm.1), custom_call_target="tpu_custom_call" | custom-call | tf_op jit(solution)/shard_map/rpa_exchange/pallas_call | solution.py:251
  54.6 1.5 %copy.9 = f32[12,1024]{1,0:T(8,128)} copy(f32[12,1024]{1,0:T(8,128)} %rpa_exchange.1) | data formatting | bytes 98304

commit v2 on v1

v2 whole, which is shorter than its diff:
```python
import jax
import jax.numpy as jnp
from jax import lax
from jax.experimental import pallas as pl
from jax.experimental.pallas import tpu as pltpu
from jax.sharding import PartitionSpec as P

MESH = pl.DeviceIdType.MESH
F32 = jnp.float32


def kernel(
    b_hbm, w_hbm, gaps_hbm, omega_hbm, weight_hbm, slot_hbm, list_hbm, out_ref,
    b_own, w_ref, gaps, omega, weight, slot, blist, in_sem,
    rows_ref, fac_ref, bg, part, part_in, ys, yq, ysc, yrq, yrs, xs, xq, xsc, xrq, xrs, zq, zsc, zrq, zrs,
    hop, g_send, g_recv, d_send, d_recv, y_send, y_recv, x_send, x_recv, z_send, z_recv,
):
    f, r, c = lax.axis_index("freq"), lax.axis_index("row"), lax.axis_index("col")
    y, zh, core = r // 4, (r // 2) % 2, r % 2
    slots = w_ref.shape[0]

    def at_x(k):
        return ((f + k) % 4, r, c)

    def at_y(k):
        return (f, (r + 4 * k) % 16, c)

    partner = (f, r + 1 - 2 * core, c)
    across = (f, r + 2 - 4 * zh, c)

    def at_z(d):
        z = (zh * 8 + c + d + 16) % 16
        return (f, r + 2 * (z // 8 - zh), z % 8)

    def tell(i, d):
        pl.semaphore_signal(hop.at[i], inc=1, device_id=at_z(d), device_id_type=MESH)

    def encode(x, to, scale):
        top = jnp.maximum(jnp.max(jnp.abs(x), axis=0, keepdims=True), 1e-30)
        to[...] = jnp.round(x * (32767.0 / top)).astype(jnp.int32).astype(jnp.int16)
        scale[...] = top * (1.0 / 32767.0)

    def decode(held, scale):
        return held[...].astype(jnp.int32).astype(F32) * scale[...]

    barrier = pltpu.get_barrier_semaphore()
    peers = [at_x(1), at_x(3), at_x(2), at_y(1), at_y(3), at_y(2), partner, at_z(1), at_z(-1)]
    for peer in peers:
        pl.semaphore_signal(barrier, inc=1, device_id=peer, device_id_type=MESH)

    small = [
        pltpu.make_async_copy(src, dst, in_sem.at[i])
        for i, (src, dst) in enumerate(
            ((list_hbm, blist), (gaps_hbm, gaps), (slot_hbm, slot), (omega_hbm, omega), (weight_hbm, weight))
        )
    ]
    own = pltpu.make_async_copy(b_hbm, b_own, in_sem.at[5])
    heavy = [pltpu.make_async_copy(w_hbm.at[s], w_ref.at[s], in_sem.at[6 + s]) for s in range(slots)]
    own.start()
    for copy in small + heavy:
        copy.start()

    to = lax.broadcasted_iota(jnp.int32, (192, 192), 0)
    source = lax.broadcasted_iota(jnp.int32, (192, 192), 1)
    half_of = (to >= 96).astype(jnp.int32)
    in_half = to - 96 * half_of
    core_of = (in_half >= 48).astype(jnp.int32)
    in_core = in_half - 48 * core_of
    tail = in_core - 32
    wide_y, wide_i = lax.shift_right_logical(in_core, 3), lax.bitwise_and(in_core, 7)
    tail_y, tail_i = lax.shift_right_logical(jnp.maximum(tail, 0), 2), 8 + lax.bitwise_and(jnp.maximum(tail, 0), 3)
    y_of = jnp.where(tail >= 0, tail_y, wide_y)
    i_of = jnp.where(tail >= 0, tail_i, wide_i)
    z_of = jnp.where(half_of == 0, 1 - zh, zh)
    wanted = y_of * 48 + z_of * 24 + core_of * 12 + i_of
    permute = jnp.where(source == wanted, 1.0, 0.0).astype(jnp.bfloat16)
    for copy in small:
        copy.wait()

    def weights(k, half):
        n = 2 * k + half
        z = 1 - zh if half == 0 else zh

        def fill(m, carry):
            of_core, of_y = m // 4, m % 4
            block = blist[((f + 4 - k) % 4) * 16 + of_y * 4 + z * 2 + of_core]
            for i in range(12):
                row = of_core * 48 + (of_y * 8 + i if i < 8 else 32 + of_y * 4 + i - 8)
                rows_ref[n, pl.ds(row, 1), :] = jnp.full((1, 128), gaps[block * 12 + i], F32)
            return carry

        with jax.named_scope(f'fill{k}{half}'):
          lax.fori_loop(0, 8, fill, 0)
          gap = rows_ref[n]
          for s in range(slots):
            held = slot[f * slots + s]
            fac_ref[s, n] = weight[held] * 2.0 * gap / (gap * gap + omega[held] * omega[held])

    own.wait()
    with jax.named_scope('permute'):
      bg[0] = jnp.dot(permute, b_own[...], preferred_element_type=F32).astype(jnp.bfloat16)
    weights(0, 0)

    with jax.named_scope('barrier'):
      pl.semaphore_wait(barrier, len(peers))

    def gather(k, half):
        rows = pl.ds(96 * half, 96)
        return pltpu.make_async_remote_copy(
            src_ref=bg.at[0, rows], dst_ref=bg.at[k, rows], send_sem=g_send.at[2 * k + half],
            recv_sem=g_recv.at[2 * k + half], device_id=at_x(k), device_id_type=MESH,
        )

    gathers = {(k, half): gather(k, half) for half in range(2) for k in (1, 3, 2)}
    for k in (1, 3, 2):
        gathers[k, 0].start()
    tell(0, -1)
    tell(1, 1)
    with jax.named_scope('w_wait'):
      for copy in heavy:
        copy.wait()

    def compute(k, half):
        left = bg[k, pl.ds(96 * half, 96), :]

        def tile(n, carry):
            columns = pl.ds(pl.multiple_of(n * 256, 256), 256)
            total = None
            for s in range(slots):
                product = jnp.dot(left, w_ref[s, :, columns], preferred_element_type=F32)
                factor = fac_ref[s, 2 * k + half]
                term = product * jnp.concatenate([factor, factor], axis=1)
                total = term if total is None else total + term
            part[2 * k + half, :, columns] = total
            return carry

        with jax.named_scope(f'compute{k}{half}'):
          lax.fori_loop(0, w_ref.shape[2] // 256, tile, 0)

    def swap(k, half):
        n = 2 * k + half
        return pltpu.make_async_remote_copy(
            src_ref=part.at[n, pl.ds(pl.multiple_of(48 - 48 * core, 8), 48)], dst_ref=part_in.at[n],
            send_sem=d_send.at[n], recv_sem=d_recv.at[n], device_id=partner, device_id_type=MESH,
        )

    def send(pairs, ssem, rsem, device):
        return [
            pltpu.make_async_remote_copy(
                src_ref=src, dst_ref=dst, send_sem=ssem.at[i], recv_sem=rsem.at[i],
                device_id=device, device_id_type=MESH,
            )
            for i, (src, dst) in enumerate(pairs)
        ]

    def along_y(k, half, j):
        n, d = 2 * k + half, (y + j) % 4
        pairs = ((yq.at[n, d], yrq.at[n, j - 1]), (ysc.at[n, d], yrs.at[n, j - 1]))
        return send(pairs, y_send.at[n, j - 1], y_recv.at[n, j - 1], at_y(j))

    def along_x(k, half):
        n = 2 * k + half
        return send(((xq.at[n], xrq.at[n]), (xsc.at[n], xrs.at[n])), x_send.at[n], x_recv.at[n], at_x(4 - k))

    low = lax.broadcasted_iota(jnp.int32, (8, 512), 0) < 4

    def to_y(k, half):
        n = 2 * k + half
        with jax.named_scope(f'wswap{k}{half}'):
          swap(k, half).wait_recv()
        with jax.named_scope(f'enc{k}{half}'):
          both = part[n, pl.ds(pl.multiple_of(48 * core, 8), 48), :] + part_in[n]
          for d in range(4):
            mixed = both[32 + 8 * (d // 2) : 40 + 8 * (d // 2)]
            if d % 2 == 0:
                mixed = jnp.where(low, mixed[:, :512], pltpu.roll(mixed[:, 512:], 4, 0))
            else:
                mixed = jnp.where(low, pltpu.roll(mixed[:, :512], 4, 0), mixed[:, 512:])
            tiles = [both[8 * d : 8 * d + 8, 256 * i : 256 * i + 256] for i in range(4)]
            piece = jnp.concatenate(tiles + [mixed[:, :256], mixed[:, 256:]], axis=0)
            ys[n, d] = piece
            encode(piece, yq.at[n, d], ysc.at[n, d])
        for j in (1, 3, 2):
            for copy in along_y(k, half, j):
                copy.start()

    def to_x(k, half):
        n = 2 * k + half
        with jax.named_scope(f'wy{k}{half}'):
          for j in (1, 3, 2):
            for copy in along_y(k, half, j):
                copy.wait_recv()
        total = ys[n, y]
        for j in range(3):
            total = total + decode(yrq.at[n, j], yrs.at[n, j])
        if k:
            encode(total, xq.at[n], xsc.at[n])
            for copy in along_x(k, half):
                copy.start()
        else:
            xs[half] = total

    def arrived(half):
        with jax.named_scope(f'wx{half}'):
          for k in (1, 3, 2):
            for copy in along_x(k, half):
                copy.wait_recv()
        total = xs[half]
        for k in (1, 2, 3):
            total = total + decode(xrq.at[2 * k + half], xrs.at[2 * k + half])
        return total

    def begin(k, half):
        if k:
            with jax.named_scope(f'wgather{k}{half}'):
              gathers[k, half].wait_recv()
        compute(k, half)
        swap(k, half).start()

    begin(0, 0)
    for k in (1, 3, 2):
        weights(k, 0)
    to_y(0, 0)
    begin(1, 0)
    pl.semaphore_wait(hop.at[0], 1)
    pl.semaphore_wait(hop.at[1], 1)
    tell(2, -2)
    tell(3, 2)
    begin(3, 0)
    to_y(1, 0)
    begin(2, 0)
    to_y(3, 0)
    for k in (1, 3, 2):
        gathers[k, 1].start()
    for k in (0, 1):
        weights(k, 1)
    to_y(2, 0)
    pl.semaphore_wait(hop.at[2], 1)
    pl.semaphore_wait(hop.at[3], 1)
    tell(4, 4)
    to_x(0, 0)
    begin(0, 1)
    to_x(1, 0)
    begin(1, 1)
    to_x(3, 0)
    to_x(2, 0)
    for k in (3, 2):
        weights(k, 1)
    begin(3, 1)
    total = arrived(0)
    with jax.named_scope('hop'):
      pl.semaphore_wait(hop.at[4], 1)
    encode(total, zq, zsc)
    over = send(((zq, zrq), (zsc, zrs)), z_send, z_recv, across)
    for copy in over:
        copy.start()
    begin(2, 1)
    for k in (0, 1, 3, 2):
        to_y(k, 1)
    for k in (0, 1, 3, 2):
        to_x(k, 1)
    kept = arrived(1)
    with jax.named_scope('wz'):
      for copy in over:
        copy.wait_recv()
    total = kept + decode(zrq, zrs)
    for i in range(4):
        out_ref[0:8, 256 * i : 256 * i + 256] = total[8 * i : 8 * i + 8]
    for i in range(2):
        mixed = total[32 + 8 * i : 40 + 8 * i]
        out_ref[8:12, 256 * i : 256 * i + 256] = mixed[0:4]
        out_ref[8:12, 512 + 256 * i : 768 + 256 * i] = pltpu.roll(mixed, 4, 0)[0:4]

    with jax.named_scope('drain'):
      for half in range(2):
        for k in range(4):
            swap(k, half).wait_send()
            for j in (1, 2, 3):
                for copy in along_y(k, half, j):
                    copy.wait_send()
            if k:
                gathers[k, half].wait_send()
                for copy in along_x(k, half):
                    copy.wait_send()
      for copy in over:
        copy.wait_send()


def local(*args):
    dma = pltpu.SemaphoreType.DMA
    hbm = pl.BlockSpec(memory_space=pl.ANY)
    pair_block, screened, pair_gaps, omega_values, quad_weight, freq_slot, block_list = args
    scratch = [
        pltpu.VMEM(pair_block.shape, jnp.bfloat16),
        pltpu.VMEM(screened.shape, jnp.bfloat16),
        pltpu.SMEM(pair_gaps.shape, F32),
        pltpu.SMEM(omega_values.shape, F32),
        pltpu.SMEM(quad_weight.shape, F32),
        pltpu.SMEM(freq_slot.shape, jnp.int32),
        pltpu.SMEM(block_list.shape, jnp.int32),
        dma((10,)),
        pltpu.VMEM((8, 96, 128), F32),
        pltpu.VMEM((4, 8, 96, 128), F32),
        pltpu.VMEM((4, 192, 512), jnp.bfloat16),
        pltpu.VMEM((8, 96, 1024), F32),
        pltpu.VMEM((8, 48, 1024), F32),
        pltpu.VMEM((8, 4, 48, 256), F32),
        pltpu.VMEM((8, 4, 48, 256), jnp.int16),
        pltpu.VMEM((8, 4, 1, 256), F32),
        pltpu.VMEM((8, 3, 48, 256), jnp.int16),
        pltpu.VMEM((8, 3, 1, 256), F32),
        pltpu.VMEM((2, 48, 256), F32),
        pltpu.VMEM((8, 48, 256), jnp.int16),
        pltpu.VMEM((8, 1, 256), F32),
        pltpu.VMEM((8, 48, 256), jnp.int16),
        pltpu.VMEM((8, 1, 256), F32),
        pltpu.VMEM((48, 256), jnp.int16),
        pltpu.VMEM((1, 256), F32),
        pltpu.VMEM((48, 256), jnp.int16),
        pltpu.VMEM((1, 256), F32),
        pltpu.SemaphoreType.REGULAR((5,)),
        dma((8,)), dma((8,)), dma((8,)), dma((8,)), dma((8, 3, 2)), dma((8, 3, 2)), dma((8, 2)), dma((8, 2)),
        dma((2,)), dma((2,)),
    ]
    return pl.pallas_call(
        kernel,
        out_shape=jax.ShapeDtypeStruct((12, 1024), F32),
        in_specs=[hbm] * 7,
        out_specs=pl.BlockSpec(memory_space=pltpu.VMEM),
        scratch_shapes=scratch,
        compiler_params=pltpu.CompilerParams(collective_id=0, has_side_effects=True),
        name="rpa_exchange",
    )(*args)


def solution(mesh):
    placed = (P("freq", "row"), P("freq", "row", "col"), P(), P(), P(), P(), P())
    return jax.shard_map(
        local, mesh=mesh, in_specs=placed, out_specs=P(("freq", "row"), "col"), check_vma=False
    )
```

time: 56.2 us -> 46.3 us (0.82)
  the two profiles are of different devices: /device:TPU:1 before, /device:TPU:2 now
where the time goes in v2:
time: 46.3 us; the launch traced here: 46.2 us
  Pallas kernels  44.7 us (97%)
  local copies, waits for them, and re-layouts  1.47 us (3%)
    pallas_call x1, Pallas kernels, local(): pl.pallas_call(kernel, out_shape=jax.ShapeDtypeStruct((12, 1024), F32), i...  44.7 us
    unnamed x1, local copies, waits for them, and re-layouts  1.47 us

profile of v2, /device:TPU:2, one launch (start us, length us, event | category | flops | bytes accessed | tf_op | source)
XLA Modules:
  0.0 46.2 jit_solution(16019204008504737147)
XLA Ops:
  0.0 44.7 %rpa_exchange.1 = f32[12,1024]{1,0:T(8,128)} custom-call(bf16[192,512]{1,0:T(8,128)(2,1)} %b_hbm.1, bf16[4,512,1024]{2,1,0:T(8,128)(2,1)} %w_hbm.1, f32[768]{0:T(1024)} %gaps_hbm.1, f32[16]{0:T(128)} %omega_hbm.1, f32[16]{0:T(128)} %weight_hbm.1, s32[16]{0:T(128)} %slot_hbm.1, s32[64]{0:T(128)} %list_hbm.1), custom_call_target="tpu_custom_call" | custom-call | tf_op jit(solution)/shard_map/rpa_exchange/pallas_call | solution.py:325
  44.7 1.5 %copy.9 = f32[12,1024]{1,0:T(8,128)} copy(f32[12,1024]{1,0:T(8,128)} %rpa_exchange.1) | data formatting | bytes 98304

commit v3 on v2

--- a/solution.py
+++ b/solution.py
@@ -120,22 +120,26 @@
       for copy in heavy:
         copy.wait()
 
-    def compute(k, half):
-        left = bg[k, pl.ds(96 * half, 96), :]
+    def compute(*blocks):
+        left = jnp.concatenate([bg[k, 96 * half : 96 * half + 96] for k, half in blocks], axis=0)
 
         def tile(n, carry):
             columns = pl.ds(pl.multiple_of(n * 256, 256), 256)
-            total = None
+            totals = [None] * len(blocks)
             for s in range(slots):
                 product = jnp.dot(left, w_ref[s, :, columns], preferred_element_type=F32)
-                factor = fac_ref[s, 2 * k + half]
-                term = product * jnp.concatenate([factor, factor], axis=1)
-                total = term if total is None else total + term
-            part[2 * k + half, :, columns] = total
+                for i, (k, half) in enumerate(blocks):
+                    factor = fac_ref[s, 2 * k + half]
+                    term = product[96 * i : 96 * i + 96] * jnp.concatenate([factor, factor], axis=1)
+                    totals[i] = term if totals[i] is None else totals[i] + term
+            for (k, half), total in zip(blocks, totals):
+                part[2 * k + half, :, columns] = total
             return carry
 
-        with jax.named_scope(f'compute{k}{half}'):
-          lax.fori_loop(0, w_ref.shape[2] // 256, tile, 0)
+        with jax.named_scope('compute' + ''.join(f'{k}{half}' for k, half in blocks)):
+            lax.fori_loop(0, w_ref.shape[2] // 256, tile, 0)
+        for block in blocks:
+            swap(*block).start()
 
     def swap(k, half):
         n = 2 * k + half
@@ -210,43 +214,43 @@
             total = total + decode(xrq.at[2 * k + half], xrs.at[2 * k + half])
         return total
 
-    def begin(k, half):
-        if k:
+    def gathered(*blocks):
+        for k, half in blocks:
             with jax.named_scope(f'wgather{k}{half}'):
-              gathers[k, half].wait_recv()
-        compute(k, half)
-        swap(k, half).start()
-
-    begin(0, 0)
+                gathers[k, half].wait_recv()
+
+    weights(0, 1)
+    compute((0, 0), (0, 1))
     for k in (1, 3, 2):
         weights(k, 0)
     to_y(0, 0)
-    begin(1, 0)
+    gathered((1, 0), (3, 0))
+    for k in (1, 3, 2):
+        gathers[k, 1].start()
+    compute((1, 0), (3, 0))
     pl.semaphore_wait(hop.at[0], 1)
     pl.semaphore_wait(hop.at[1], 1)
     tell(2, -2)
     tell(3, 2)
-    begin(3, 0)
+    to_y(0, 1)
+    gathered((2, 0))
+    compute((2, 0))
     to_y(1, 0)
-    begin(2, 0)
     to_y(3, 0)
     for k in (1, 3, 2):
-        gathers[k, 1].start()
-    for k in (0, 1):
         weights(k, 1)
     to_y(2, 0)
     pl.semaphore_wait(hop.at[2], 1)
     pl.semaphore_wait(hop.at[3], 1)
     tell(4, 4)
     to_x(0, 0)
-    begin(0, 1)
+    gathered((1, 1), (3, 1), (2, 1))
+    compute((1, 1), (3, 1), (2, 1))
     to_x(1, 0)
-    begin(1, 1)
     to_x(3, 0)
     to_x(2, 0)
-    for k in (3, 2):
-        weights(k, 1)
-    begin(3, 1)
+    for k in (1, 3, 2):
+        to_y(k, 1)
     total = arrived(0)
     with jax.named_scope('hop'):
       pl.semaphore_wait(hop.at[4], 1)
@@ -254,9 +258,6 @@
     over = send(((zq, zrq), (zsc, zrs)), z_send, z_recv, across)
     for copy in over:
         copy.start()
-    begin(2, 1)
-    for k in (0, 1, 3, 2):
-        to_y(k, 1)
     for k in (0, 1, 3, 2):
         to_x(k, 1)
     kept = arrived(1)
@@ -288,7 +289,7 @@
 
 def local(*args):
     dma = pltpu.SemaphoreType.DMA
-    hbm = pl.BlockSpec(memory_space=pl.ANY)
+    hbm = pl.BlockSpec(memory_space=pltpu.HBM)
     pair_block, screened, pair_gaps, omega_values, quad_weight, freq_slot, block_list = args
     scratch = [
         pltpu.VMEM(pair_block.shape, jnp.bfloat16),
@@ -328,9 +329,9 @@
         in_specs=[hbm] * 7,
         out_specs=pl.BlockSpec(memory_space=pltpu.VMEM),
         scratch_shapes=scratch,
-        compiler_params=pltpu.CompilerParams(collective_id=0, has_side_effects=True),
+        compiler_params=pltpu.CompilerParams(collective_id=0, has_side_effects=True, vmem_limit_bytes=20 << 20),
         name="rpa_exchange",
-    )(*args)
+    )(*(pltpu.with_memory_space_constraint(a, pltpu.HBM) for a in args))
 
 
 def solution(mesh):

time: 46.3 us -> 40.5 us (0.87)
  Pallas kernels: 44.7 us -> 39.8 us
  local copies, waits for them, and re-layouts: 1.47 us -> 0.63 us
    pallas_call x1, Pallas kernels: 44.7 us -> 39.8 us  [local(): pl.pallas_call(kernel, out_shape=jax.ShapeDtypeStruct((12, 1024), F32), i...]
    unnamed x1, local copies, waits for them, and re-layouts: 1.47 us -> 0.63 us
where the time goes in v3:
time: 40.5 us; the launch traced here: 40.4 us
  Pallas kernels  39.8 us (98%)
  local copies, waits for them, and re-layouts  0.63 us (2%)
    pallas_call x1, Pallas kernels, local(): pl.pallas_call(kernel, out_shape=jax.ShapeDtypeStruct((12, 1024), F32), i...  39.8 us

profile of v3, /device:TPU:2, one launch (start us, length us, event | category | flops | bytes accessed | tf_op | source)
XLA Modules:
  0.0 40.4 jit_solution(6890197727529414191)
XLA Ops:
  0.0 39.8 %rpa_exchange.1 = f32[12,1024]{1,0:T(8,128)S(1)} custom-call(bf16[192,512]{1,0:T(8,128)(2,1)} %b_hbm.1, bf16[4,512,1024]{2,1,0:T(8,128)(2,1)} %w_hbm.1, f32[768]{0:T(1024)} %gaps_hbm.1, f32[16]{0:T(128)} %omega_hbm.1, f32[16]{0:T(128)} %weight_hbm.1, s32[16]{0:T(128)} %slot_hbm.1, s32[64]{0:T(128)} %list_hbm.1), custom_call_target="tpu_custom_call" | custom-call | tf_op jit(solution)/shard_map/rpa_exchange/pallas_call | solution.py:326
  39.8 0.6 %copy.9 = f32[12,1024]{1,0:T(8,128)} copy(f32[12,1024]{1,0:T(8,128)S(1)} %rpa_exchange.1) | data formatting | bytes 98304

commit v4 on v3

--- a/solution.py
+++ b/solution.py
@@ -43,10 +43,44 @@
     def decode(held, scale):
         return held[...].astype(jnp.int32).astype(F32) * scale[...]
 
+    zpos = zh * 8 + c
     barrier = pltpu.get_barrier_semaphore()
-    peers = [at_x(1), at_x(3), at_x(2), at_y(1), at_y(3), at_y(2), partner, at_z(1), at_z(-1)]
+    peers = [at_x(1), at_x(3), at_x(2), at_y(1), at_y(3), at_y(2), partner]
     for peer in peers:
         pl.semaphore_signal(barrier, inc=1, device_id=peer, device_id_type=MESH)
+    for d, there in ((1, zpos < 15), (-1, zpos > 0)):
+
+        @pl.when(there)
+        def _():
+            pl.semaphore_signal(barrier, inc=1, device_id=at_z(d), device_id_type=MESH)
+
+    def between(low, high):
+        return pl.when(jnp.logical_and(zpos >= low, zpos <= high))
+
+    def learn(step):
+        if step == 1:
+            between(1, 12)(lambda: tell(0, 1))
+            between(3, 14)(lambda: tell(1, -1))
+        elif step == 2:
+
+            @between(2, 13)
+            def _():
+                pl.semaphore_wait(hop.at[0], 1)
+                pl.semaphore_wait(hop.at[1], 1)
+
+            between(2, 9)(lambda: tell(2, 2))
+            between(6, 13)(lambda: tell(3, -2))
+        elif step == 3:
+
+            @between(4, 11)
+            def _():
+                pl.semaphore_wait(hop.at[2], 1)
+                pl.semaphore_wait(hop.at[3], 1)
+                tell(4, 4)
+                tell(4, -4)
+
+        else:
+            pl.semaphore_wait(hop.at[4], 1)
 
     small = [
         pltpu.make_async_copy(src, dst, in_sem.at[i])
@@ -102,25 +136,24 @@
     weights(0, 0)
 
     with jax.named_scope('barrier'):
-      pl.semaphore_wait(barrier, len(peers))
+      pl.semaphore_wait(barrier, len(peers) + (zpos < 15).astype(jnp.int32) + (zpos > 0).astype(jnp.int32))
 
     def gather(k, half):
         rows = pl.ds(96 * half, 96)
         return pltpu.make_async_remote_copy(
-            src_ref=bg.at[0, rows], dst_ref=bg.at[k, rows], send_sem=g_send.at[2 * k + half],
+            src_ref=bg.at[0, rows], dst_ref=bg.at[k, rows], send_sem=g_send,
             recv_sem=g_recv.at[2 * k + half], device_id=at_x(k), device_id_type=MESH,
         )
 
     gathers = {(k, half): gather(k, half) for half in range(2) for k in (1, 3, 2)}
     for k in (1, 3, 2):
         gathers[k, 0].start()
-    tell(0, -1)
-    tell(1, 1)
+    learn(1)
     with jax.named_scope('w_wait'):
       for copy in heavy:
         copy.wait()
 
-    def compute(*blocks):
+    def compute(blocks, h):
         left = jnp.concatenate([bg[k, 96 * half : 96 * half + 96] for k, half in blocks], axis=0)
 
         def tile(n, carry):
@@ -137,15 +170,17 @@
             return carry
 
         with jax.named_scope('compute' + ''.join(f'{k}{half}' for k, half in blocks)):
-            lax.fori_loop(0, w_ref.shape[2] // 256, tile, 0)
-        for block in blocks:
-            swap(*block).start()
-
-    def swap(k, half):
-        n = 2 * k + half
+            lax.fori_loop(2 * h, 2 * h + 2, tile, 0)
+        for k, half in blocks:
+            swap(k, half, h).start()
+
+    def swap(k, half, h):
+        n = 2 * k + half
+        columns = pl.ds(512 * h, 512)
         return pltpu.make_async_remote_copy(
-            src_ref=part.at[n, pl.ds(pl.multiple_of(48 - 48 * core, 8), 48)], dst_ref=part_in.at[n],
-            send_sem=d_send.at[n], recv_sem=d_recv.at[n], device_id=partner, device_id_type=MESH,
+            src_ref=part.at[n, pl.ds(pl.multiple_of(48 - 48 * core, 8), 48), columns],
+            dst_ref=part_in.at[n, :, columns], send_sem=d_send, recv_sem=d_recv.at[n, h],
+            device_id=partner, device_id_type=MESH,
         )
 
     def send(pairs, ssem, rsem, device):
@@ -157,61 +192,67 @@
             for i, (src, dst) in enumerate(pairs)
         ]
 
-    def along_y(k, half, j):
+    def landed(ref, sem):
+        pltpu.make_async_copy(ref, ref, sem).wait()
+
+    def along_y(k, half, h, j):
         n, d = 2 * k + half, (y + j) % 4
-        pairs = ((yq.at[n, d], yrq.at[n, j - 1]), (ysc.at[n, d], yrs.at[n, j - 1]))
-        return send(pairs, y_send.at[n, j - 1], y_recv.at[n, j - 1], at_y(j))
-
-    def along_x(k, half):
-        n = 2 * k + half
-        return send(((xq.at[n], xrq.at[n]), (xsc.at[n], xrs.at[n])), x_send.at[n], x_recv.at[n], at_x(4 - k))
-
-    low = lax.broadcasted_iota(jnp.int32, (8, 512), 0) < 4
-
-    def to_y(k, half):
-        n = 2 * k + half
-        with jax.named_scope(f'wswap{k}{half}'):
-          swap(k, half).wait_recv()
-        with jax.named_scope(f'enc{k}{half}'):
-          both = part[n, pl.ds(pl.multiple_of(48 * core, 8), 48), :] + part_in[n]
-          for d in range(4):
+        pairs = ((yq.at[n, h, d], yrq.at[n, h, j - 1]), (ysc.at[n, h, d], yrs.at[n, h, j - 1]))
+        return send(pairs, y_send, y_recv.at[n, h], at_y(j))
+
+    def along_x(k, half, h):
+        n = 2 * k + half
+        pairs = ((xq.at[n, h], xrq.at[half, h, k - 1]), (xsc.at[n, h], xrs.at[half, h, k - 1]))
+        return send(pairs, x_send, x_recv.at[half, h], at_x(4 - k))
+
+    def along_z(h):
+        pairs = ((zq.at[h], zrq.at[h]), (zsc.at[h], zrs.at[h]))
+        return send(pairs, z_send, z_recv.at[h], across)
+
+    low = lax.broadcasted_iota(jnp.int32, (8, 256), 0) < 4
+
+    def to_y(k, half, h):
+        n = 2 * k + half
+        with jax.named_scope(f'wswap{k}{half}{h}'):
+            swap(k, half, h).wait_recv()
+        columns = pl.ds(512 * h, 512)
+        both = part[n, pl.ds(pl.multiple_of(48 * core, 8), 48), columns] + part_in[n, :, columns]
+        for d in range(4):
             mixed = both[32 + 8 * (d // 2) : 40 + 8 * (d // 2)]
             if d % 2 == 0:
-                mixed = jnp.where(low, mixed[:, :512], pltpu.roll(mixed[:, 512:], 4, 0))
+                mixed = jnp.where(low, mixed[:, :256], pltpu.roll(mixed[:, 256:], 4, 0))
             else:
-                mixed = jnp.where(low, pltpu.roll(mixed[:, :512], 4, 0), mixed[:, 512:])
-            tiles = [both[8 * d : 8 * d + 8, 256 * i : 256 * i + 256] for i in range(4)]
-            piece = jnp.concatenate(tiles + [mixed[:, :256], mixed[:, 256:]], axis=0)
-            ys[n, d] = piece
-            encode(piece, yq.at[n, d], ysc.at[n, d])
+                mixed = jnp.where(low, pltpu.roll(mixed[:, :256], 4, 0), mixed[:, 256:])
+            tiles = [both[8 * d : 8 * d + 8, 128 * i : 128 * i + 128] for i in range(4)]
+            piece = jnp.concatenate(tiles + [mixed[:, :128], mixed[:, 128:]], axis=0)
+            ys[n, h, d] = piece
+            encode(piece, yq.at[n, h, d], ysc.at[n, h, d])
         for j in (1, 3, 2):
-            for copy in along_y(k, half, j):
+            for copy in along_y(k, half, h, j):
                 copy.start()
 
-    def to_x(k, half):
-        n = 2 * k + half
-        with jax.named_scope(f'wy{k}{half}'):
-          for j in (1, 3, 2):
-            for copy in along_y(k, half, j):
-                copy.wait_recv()
-        total = ys[n, y]
+    def to_x(k, half, h):
+        n = 2 * k + half
+        with jax.named_scope(f'wy{k}{half}{h}'):
+            landed(yrq.at[n, h], y_recv.at[n, h, 0])
+            landed(yrs.at[n, h], y_recv.at[n, h, 1])
+        total = ys[n, h, y]
         for j in range(3):
-            total = total + decode(yrq.at[n, j], yrs.at[n, j])
+            total = total + decode(yrq.at[n, h, j], yrs.at[n, h, j])
         if k:
-            encode(total, xq.at[n], xsc.at[n])
-            for copy in along_x(k, half):
+            encode(total, xq.at[n, h], xsc.at[n, h])
+            for copy in along_x(k, half, h):
                 copy.start()
         else:
-            xs[half] = total
-
-    def arrived(half):
-        with jax.named_scope(f'wx{half}'):
-          for k in (1, 3, 2):
-            for copy in along_x(k, half):
-                copy.wait_recv()
-        total = xs[half]
-        for k in (1, 2, 3):
-            total = total + decode(xrq.at[2 * k + half], xrs.at[2 * k + half])
+            xs[half, h] = total
+
+    def arrived(half, h):
+        with jax.named_scope(f'wx{half}{h}'):
+            landed(xrq.at[half, h], x_recv.at[half, h, 0])
+            landed(xrs.at[half, h], x_recv.at[half, h, 1])
+        total = xs[half, h]
+        for k in range(3):
+            total = total + decode(xrq.at[half, h, k], xrs.at[half, h, k])
         return total
 
     def gathered(*blocks):
@@ -220,71 +261,77 @@
                 gathers[k, half].wait_recv()
 
     weights(0, 1)
-    compute((0, 0), (0, 1))
+    for h in range(2):
+        compute(((0, 0), (0, 1)), h)
     for k in (1, 3, 2):
         weights(k, 0)
-    to_y(0, 0)
+    for h in range(2):
+        to_y(0, 0, h)
     gathered((1, 0), (3, 0))
     for k in (1, 3, 2):
         gathers[k, 1].start()
-    compute((1, 0), (3, 0))
-    pl.semaphore_wait(hop.at[0], 1)
-    pl.semaphore_wait(hop.at[1], 1)
-    tell(2, -2)
-    tell(3, 2)
-    to_y(0, 1)
+    for h in range(2):
+        compute(((1, 0), (3, 0)), h)
+    learn(2)
+    for h in range(2):
+        to_y(0, 1, h)
     gathered((2, 0))
-    compute((2, 0))
-    to_y(1, 0)
-    to_y(3, 0)
+    for h in range(2):
+        compute(((2, 0),), h)
+        to_y(1, 0, h)
+        to_y(3, 0, h)
+    for h in range(2):
+        to_y(2, 0, h)
     for k in (1, 3, 2):
         weights(k, 1)
-    to_y(2, 0)
-    pl.semaphore_wait(hop.at[2], 1)
-    pl.semaphore_wait(hop.at[3], 1)
-    tell(4, 4)
-    to_x(0, 0)
+    learn(3)
+    for h in range(2):
+        to_x(0, 0, h)
     gathered((1, 1), (3, 1), (2, 1))
-    compute((1, 1), (3, 1), (2, 1))
-    to_x(1, 0)
-    to_x(3, 0)
-    to_x(2, 0)
-    for k in (1, 3, 2):
-        to_y(k, 1)
-    total = arrived(0)
+    home = ((1, 1), (3, 1), (2, 1))
+    compute(home, 0)
+    for h in range(2):
+        for k in (1, 3):
+            to_x(k, 0, h)
+    for h in range(2):
+        to_x(2, 0, h)
+    compute(home, 1)
+    for k, half in home:
+        to_y(k, half, 0)
     with jax.named_scope('hop'):
-      pl.semaphore_wait(hop.at[4], 1)
-    encode(total, zq, zsc)
-    over = send(((zq, zrq), (zsc, zrs)), z_send, z_recv, across)
-    for copy in over:
-        copy.start()
-    for k in (0, 1, 3, 2):
-        to_x(k, 1)
-    kept = arrived(1)
-    with jax.named_scope('wz'):
-      for copy in over:
-        copy.wait_recv()
-    total = kept + decode(zrq, zrs)
-    for i in range(4):
-        out_ref[0:8, 256 * i : 256 * i + 256] = total[8 * i : 8 * i + 8]
-    for i in range(2):
-        mixed = total[32 + 8 * i : 40 + 8 * i]
-        out_ref[8:12, 256 * i : 256 * i + 256] = mixed[0:4]
-        out_ref[8:12, 512 + 256 * i : 768 + 256 * i] = pltpu.roll(mixed, 4, 0)[0:4]
+        learn(4)
+    for h in range(2):
+        encode(arrived(0, h), zq.at[h], zsc.at[h])
+        for copy in along_z(h):
+            copy.start()
+    for k, half in home:
+        to_y(k, half, 1)
+    for h in range(2):
+        for k in (0, 1, 3, 2):
+            to_x(k, 1, h)
+    for h in range(2):
+        kept = arrived(1, h)
+        with jax.named_scope(f'wz{h}'):
+            for copy in along_z(h):
+                copy.wait_recv()
+        total = kept + decode(zrq.at[h], zrs.at[h])
+        for i in range(4):
+            out_ref[0:8, 512 * h + 128 * i : 512 * h + 128 * i + 128] = total[8 * i : 8 * i + 8]
+        for i in range(2):
+            mixed = total[32 + 8 * i : 40 + 8 * i]
+            at = 512 * h + 128 * i
+            out_ref[8:12, at : at + 128] = mixed[0:4]
+            out_ref[8:12, at + 256 : at + 384] = pltpu.roll(mixed, 4, 0)[0:4]
 
     with jax.named_scope('drain'):
-      for half in range(2):
-        for k in range(4):
-            swap(k, half).wait_send()
-            for j in (1, 2, 3):
-                for copy in along_y(k, half, j):
-                    copy.wait_send()
-            if k:
-                gathers[k, half].wait_send()
-                for copy in along_x(k, half):
-                    copy.wait_send()
-      for copy in over:
-        copy.wait_send()
+        landed(bg.at[pl.ds(1, 3)], g_send)
+        landed(part_in, d_send)
+        landed(yrq, y_send.at[0])
+        landed(yrs, y_send.at[1])
+        landed(xrq, x_send.at[0])
+        landed(xrs, x_send.at[1])
+        landed(zrq, z_send.at[0])
+        landed(zrs, z_send.at[1])
 
 
 def local(*args):
@@ -305,23 +352,23 @@
         pltpu.VMEM((4, 192, 512), jnp.bfloat16),
         pltpu.VMEM((8, 96, 1024), F32),
         pltpu.VMEM((8, 48, 1024), F32),
-        pltpu.VMEM((8, 4, 48, 256), F32),
-        pltpu.VMEM((8, 4, 48, 256), jnp.int16),
-        pltpu.VMEM((8, 4, 1, 256), F32),
-        pltpu.VMEM((8, 3, 48, 256), jnp.int16),
-        pltpu.VMEM((8, 3, 1, 256), F32),
-        pltpu.VMEM((2, 48, 256), F32),
-        pltpu.VMEM((8, 48, 256), jnp.int16),
-        pltpu.VMEM((8, 1, 256), F32),
-        pltpu.VMEM((8, 48, 256), jnp.int16),
-        pltpu.VMEM((8, 1, 256), F32),
-        pltpu.VMEM((48, 256), jnp.int16),
-        pltpu.VMEM((1, 256), F32),
-        pltpu.VMEM((48, 256), jnp.int16),
-        pltpu.VMEM((1, 256), F32),
+        pltpu.VMEM((8, 2, 4, 48, 128), F32),
+        pltpu.VMEM((8, 2, 4, 48, 128), jnp.int16),
+        pltpu.VMEM((8, 2, 4, 1, 128), F32),
+        pltpu.VMEM((8, 2, 3, 48, 128), jnp.int16),
+        pltpu.VMEM((8, 2, 3, 1, 128), F32),
+        pltpu.VMEM((2, 2, 48, 128), F32),
+        pltpu.VMEM((8, 2, 48, 128), jnp.int16),
+        pltpu.VMEM((8, 2, 1, 128), F32),
+        pltpu.VMEM((2, 2, 3, 48, 128), jnp.int16),
+        pltpu.VMEM((2, 2, 3, 1, 128), F32),
+        pltpu.VMEM((2, 48, 128), jnp.int16),
+        pltpu.VMEM((2, 1, 128), F32),
+        pltpu.VMEM((2, 48, 128), jnp.int16),
+        pltpu.VMEM((2, 1, 128), F32),
         pltpu.SemaphoreType.REGULAR((5,)),
-        dma((8,)), dma((8,)), dma((8,)), dma((8,)), dma((8, 3, 2)), dma((8, 3, 2)), dma((8, 2)), dma((8, 2)),
-        dma((2,)), dma((2,)),
+        dma, dma((8,)), dma, dma((8, 2)), dma((2,)), dma((8, 2, 2)),
+        dma((2,)), dma((2, 2, 2)), dma((2,)), dma((2, 2)),
     ]
     return pl.pallas_call(
         kernel,

time: 40.5 us -> 39 us (0.963)
  Pallas kernels: 39.8 us -> 38.3 us
    pallas_call x1, Pallas kernels: 39.8 us -> 38.3 us  [local(): pl.pallas_call(kernel, out_shape=jax.ShapeDtypeStruct((12, 1024), F32), i...]
where the time goes in v4:
time: 39 us; the launch traced here: 38.9 us
  Pallas kernels  38.3 us (98%)
  local copies, waits for them, and re-layouts  0.63 us (2%)
    pallas_call x1, Pallas kernels, local(): pl.pallas_call(kernel, out_shape=jax.ShapeDtypeStruct((12, 1024), F32), i...  38.3 us

profile of v4, /device:TPU:2, one launch (start us, length us, event | category | flops | bytes accessed | tf_op | source)
XLA Modules:
  0.0 38.9 jit_solution(9401007172703839919)
XLA Ops:
  0.0 38.3 %rpa_exchange.1 = f32[12,1024]{1,0:T(8,128)S(1)} custom-call(bf16[192,512]{1,0:T(8,128)(2,1)} %b_hbm.1, bf16[4,512,1024]{2,1,0:T(8,128)(2,1)} %w_hbm.1, f32[768]{0:T(1024)} %gaps_hbm.1, f32[16]{0:T(128)} %omega_hbm.1, f32[16]{0:T(128)} %weight_hbm.1, s32[16]{0:T(128)} %slot_hbm.1, s32[64]{0:T(128)} %list_hbm.1), custom_call_target="tpu_custom_call" | custom-call | tf_op jit(solution)/shard_map/rpa_exchange/pallas_call | solution.py:373
  38.3 0.6 %copy.9 = f32[12,1024]{1,0:T(8,128)} copy(f32[12,1024]{1,0:T(8,128)S(1)} %rpa_exchange.1) | data formatting | bytes 98304

commit v5 on v4

--- a/solution.py
+++ b/solution.py
@@ -268,18 +268,18 @@
     for h in range(2):
         to_y(0, 0, h)
     gathered((1, 0), (3, 0))
+    for h in range(2):
+        compute(((1, 0), (3, 0)), h)
+    learn(2)
+    to_y(1, 0, 0)
+    to_y(3, 0, 0)
+    gathered((2, 0))
     for k in (1, 3, 2):
         gathers[k, 1].start()
-    for h in range(2):
-        compute(((1, 0), (3, 0)), h)
-    learn(2)
-    for h in range(2):
-        to_y(0, 1, h)
-    gathered((2, 0))
-    for h in range(2):
-        compute(((2, 0),), h)
-        to_y(1, 0, h)
-        to_y(3, 0, h)
+    compute(((2, 0),), 0)
+    to_y(1, 0, 1)
+    to_y(3, 0, 1)
+    compute(((2, 0),), 1)
     for h in range(2):
         to_y(2, 0, h)
     for k in (1, 3, 2):
@@ -287,25 +287,26 @@
     learn(3)
     for h in range(2):
         to_x(0, 0, h)
-    gathered((1, 1), (3, 1), (2, 1))
     home = ((1, 1), (3, 1), (2, 1))
-    compute(home, 0)
     for h in range(2):
         for k in (1, 3):
             to_x(k, 0, h)
     for h in range(2):
         to_x(2, 0, h)
-    compute(home, 1)
-    for k, half in home:
-        to_y(k, half, 0)
+    for h in range(2):
+        to_y(0, 1, h)
+    gathered(*home)
+    compute(home, 0)
     with jax.named_scope('hop'):
         learn(4)
     for h in range(2):
         encode(arrived(0, h), zq.at[h], zsc.at[h])
         for copy in along_z(h):
             copy.start()
-    for k, half in home:
-        to_y(k, half, 1)
+    compute(home, 1)
+    for h in range(2):
+        for k, half in home:
+            to_y(k, half, h)
     for h in range(2):
         for k in (0, 1, 3, 2):
             to_x(k, 1, h)

time: 39 us -> 38.6 us (0.990)
  Pallas kernels: 38.3 us -> 37.8 us
    pallas_call x1, Pallas kernels: 38.3 us -> 37.8 us  [local(): pl.pallas_call(kernel, out_shape=jax.ShapeDtypeStruct((12, 1024), F32), i...]
where the time goes in v5:
time: 38.6 us; the launch traced here: 38.5 us
  Pallas kernels  37.8 us (98%)
  local copies, waits for them, and re-layouts  0.63 us (2%)
    pallas_call x1, Pallas kernels, local(): pl.pallas_call(kernel, out_shape=jax.ShapeDtypeStruct((12, 1024), F32), i...  37.8 us

profile of v5, /device:TPU:2, one launch (start us, length us, event | category | flops | bytes accessed | tf_op | source)
XLA Modules:
  0.0 38.5 jit_solution(3638362618150538672)
XLA Ops:
  0.0 37.8 %rpa_exchange.1 = f32[12,1024]{1,0:T(8,128)S(1)} custom-call(bf16[192,512]{1,0:T(8,128)(2,1)} %b_hbm.1, bf16[4,512,1024]{2,1,0:T(8,128)(2,1)} %w_hbm.1, f32[768]{0:T(1024)} %gaps_hbm.1, f32[16]{0:T(128)} %omega_hbm.1, f32[16]{0:T(128)} %weight_hbm.1, s32[16]{0:T(128)} %slot_hbm.1, s32[64]{0:T(128)} %list_hbm.1), custom_call_target="tpu_custom_call" | custom-call | tf_op jit(solution)/shard_map/rpa_exchange/pallas_call | solution.py:374
  37.9 0.6 %copy.9 = f32[12,1024]{1,0:T(8,128)} copy(f32[12,1024]{1,0:T(8,128)S(1)} %rpa_exchange.1) | data formatting | bytes 98304
